TPU v7x, 32 devices: a whole 2x2x4 slice. The times are simulated.
32 devices in a mesh: rep: 4 (over x, core), grp: 8 (over z, y).
Axes of the slice: x: 2, y: 2, z: 4, core: 2. Of those that a mesh axis runs over, the one named last changes fastest.
Arguments:
- tokens: bfloat16 [8192, 2304], P(('rep', 'grp')), may hold values from -6 to 6
- norm_gain: float32 [2304], replicated, may hold values from 0.25 to 1.75
- key_weight: bfloat16 [2304, 1024], P('grp'), may hold values from -0.125 to 0.125
- key_grad: bfloat16 [8192, 1024], P(('rep', 'grp')), may hold values from -6 to 6
Outputs:
- token_grad: bfloat16 [8192, 2304], P(('rep', 'grp'))
- weight_grad: float32 [2304, 1024], P('grp', 'rep')
- gain_grad: float32 [2304], replicated
All inputs are finite; a program needn't handle non-finite values.
Results may differ from a plain program's by a relative error of at most 0.023.
Values may be sent and summed in bfloat16 or wider, within the bound.
No kernel may reach another device: no remote copies, remote signals or barrier semaphores. Data moves between devices by JAX's collectives and lax.ppermute only.
A program may use at most 64 MiB of HBM per device.

v0:
```python
import jax
import jax.numpy as jnp
from jax import lax
from jax.sharding import PartitionSpec as P

epsilon = 1e-06


def shards(tokens, norm_gain, key_weight, key_grad):
    total_tokens = tokens.shape[0] * lax.axis_size("rep") * lax.axis_size("grp")
    grad_scale = total_tokens ** (-0.5)
    wide_tokens = tokens.astype(jnp.float32)
    inv_rms = lax.rsqrt(jnp.mean(wide_tokens * wide_tokens, axis=1, keepdims=True) + epsilon)
    normed = (wide_tokens * inv_rms * norm_gain).astype(jnp.bfloat16)
    partial_value = lax.dot_general(
        normed, key_grad, (((0,), (0,)), ((), ())), preferred_element_type=jnp.float32
    )
    d_normed = lax.dot_general(
        key_grad,
        lax.all_gather(key_weight, "grp", axis=0, tiled=True),
        (((1,), (1,)), ((), ())),
        preferred_element_type=jnp.float32,
    )
    section_one = lax.psum_scatter(
        partial_value.astype(jnp.bfloat16), "rep", scatter_dimension=1, tiled=True
    ).astype(jnp.float32)
    weight_sum = lax.psum_scatter(section_one, "grp", scatter_dimension=0, tiled=True)
    gain_local = jnp.sum(d_normed * wide_tokens * inv_rms, axis=0)
    gain_total = lax.psum(gain_local, ("rep", "grp"))
    scaled = d_normed * norm_gain
    inner_mean = jnp.mean(scaled * wide_tokens, axis=1, keepdims=True)
    token_grad = (inv_rms * (scaled - wide_tokens * inv_rms * inv_rms * inner_mean)).astype(
        jnp.bfloat16
    )
    return (token_grad, weight_sum * grad_scale, gain_total * grad_scale)


def solution(mesh):
    in_specs = (P(("rep", "grp"), None), P(), P("grp", None), P(("rep", "grp"), None))
    out_specs = (P(("rep", "grp"), None), P("grp", "rep"), P())
    return jax.shard_map(shards, mesh=mesh, in_specs=in_specs, out_specs=out_specs, check_vma=False)
```

profile of v0, /device:TPU:0, one launch (start us, length us, event | category | flops | bytes accessed | tf_op | source)
XLA Modules:
  0.0 180.5 jit_solution(7372656190298099384)
XLA Ops:
  8.0 0.0 copy-start
  8.0 0.0 reduce-scatter.3.cloned.1.call-start
  8.1 1.6 fusion.7
  9.7 0.0 copy-done
  9.7 5.0 %convolution_convert_fusion = bf16[2304,1024]{1,0:T(8,128)(2,1)} fusion(bf16[256,1024]{1,0:T(8,128)(2,1)S(1)} %copy-done, bf16[256,2304]{1,0:T(8,128)(2,1)} %param.4, f32[2304]{0:T(1024)} %param.5, f32[256]{0:T(256)S(1)} %add_rsqrt_fusion), kind=kOutput, calls=%fused_computation | convolution fusion | flops 1212678144 | bytes 6432768 | tf_op jit(solution)/shard_map/dot_general | solution.py:15
  14.7 0.0 reduce-scatter.3.cloned.1.call-update
  14.7 0.0 all-gather.2.cloned.1.call-start
  14.8 0.5 all-gather.2.cloned.1.call-update
  15.3 0.0 copy-start.1
  15.3 0.0 copy-start.2
  15.3 0.0 reduce-scatter.5.cloned.1.call-start
  15.4 50.0 %reduce-scatter.3.cloned.1.call-done = bf16[2304,256]{1,0:T(8,128)(2,1)} async-done(((bf16[2304,1024]{1,0:T(8,128)(2,1)}), bf16[2304,256]{1,0:T(8,128)(2,1)}) %reduce-scatter.3.cloned.1.call-update) | async-done | bytes 1179664 | tf_op jit(solution)/shard_map/reduce_scatter | solution.py:24
  65.3 2.9 %convert_element_type.19 = f32[2304,256]{1,0:T(8,128)} convert(bf16[2304,256]{1,0:T(8,128)(2,1)} %reduce-scatter.3.cloned.1.call-done) | non-fusion elementwise | flops 589824 | bytes 3538944 | tf_op jit(solution)/shard_map/convert_element_type | solution.py:26
  68.3 0.0 reduce-scatter.5.cloned.1.call-update
  68.3 30.9 %all-gather.2.cloned.1.call-done = bf16[2304,1024]{1,0:T(8,128)(2,1)} async-done(((bf16[288,1024]{1,0:T(8,128)(2,1)}), bf16[2304,1024]{1,0:T(8,128)(2,1)}) %all-gather.2.cloned.1.call-update) | async-done | bytes 4718608 | tf_op jit(solution)/shard_map/all_gather | solution.py:20
  99.2 0.0 copy-done.1
  99.2 0.0 copy-done.2
  99.2 5.6 %fusion.10 = (f32[2304]{0:T(1024)S(1)}, f32[256]{0:T(256)S(1)}, f32[256,2304]{1,0:T(8,128)}) fusion(bf16[256,2304]{1,0:T(8,128)(2,1)S(1)} %copy-done.1, f32[256]{0:T(256)S(1)} %add_rsqrt_fusion, f32[2304]{0:T(1024)S(1)} %copy-done.2, bf16[256,1024]{1,0:T(8,128)(2,1)S(1)} %copy-done, bf16[2304,1024]{1,0:T(8,128)(2,1)} %all-gather.2.cloned.1.call-done), kind=kOutput, calls=%fused_computation.15 | convolution fusion | flops 1212085760 | bytes 8802304 | tf_op jit(solution)/shard_map/dot_general | solution.py:18
  104.8 39.4 %psum.7 = f32[2304]{0:T(1024)S(1)} all-reduce(f32[2304]{0:T(1024)S(1)} %get-tuple-element.3), channel_id=1, replica_groups=mesh['rep'=4,'grp'=8] {'rep','grp'}, use_global_device_ids=true, to_apply=%region_5.0 | all-reduce | flops 2304 | bytes 18432 | tf_op jit(solution)/shard_map/psum | solution.py:29
  144.2 0.6 broadcast_multiply_fusion.1
  144.8 3.4 %fusion.5 = bf16[256,2304]{1,0:T(8,128)(2,1)} fusion(bf16[256,2304]{1,0:T(8,128)(2,1)S(1)} %copy-done.1, f32[256,2304]{1,0:T(8,128)} %get-tuple-element.5, f32[256]{0:T(256)S(1)} %broadcast_multiply_fusion.2, f32[2304]{0:T(1024)S(1)} %copy-done.2, f32[256]{0:T(256)S(1)} %add_rsqrt_fusion), kind=kLoop, calls=%fused_computation.10 | loop fusion | flops 4718592 | bytes 4729856 | tf_op jit(solution)/shard_map/convert_element_type | solution.py:32
  148.2 23.2 %reduce-scatter.5.cloned.1.call-done = f32[288,256]{1,0:T(8,128)} async-done(((f32[2304,256]{1,0:T(8,128)}), f32[288,256]{1,0:T(8,128)}) %reduce-scatter.5.cloned.1.call-update) | async-done | bytes 294928 | tf_op jit(solution)/shard_map/reduce_scatter | solution.py:27
  171.4 1.7 broadcast_multiply_fusion
  (2 shorter events, 0.0 us)
Async XLA Ops:
  8.0 1.7 copy-start
  8.0 57.3 %reduce-scatter.3.cloned.1.call-start = ((), (), s32[]{:S(2)}) async-start(), calls=%async_computation.3 | async-start | bytes 5898240 | tf_op jit(solution)/shard_map/reduce_scatter | solution.py:24
  14.7 84.5 %all-gather.2.cloned.1.call-start = ((), (), s32[]{:S(2)}) async-start(), calls=%async_computation.2 | async-start | bytes 5308416 | tf_op jit(solution)/shard_map/all_gather | solution.py:20
  15.3 83.9 %copy-start.1 = (bf16[256,2304]{1,0:T(8,128)(2,1)S(1)}, bf16[256,2304]{1,0:T(8,128)(2,1)}, u32[]{:S(2)}) copy-start(bf16[256,2304]{1,0:T(8,128)(2,1)} %param.4) | copy-start | bytes 3538948
  15.3 83.9 %copy-start.2 = (f32[2304]{0:T(1024)S(1)}, f32[2304]{0:T(1024)}, u32[]{:S(2)}) copy-start(f32[2304]{0:T(1024)} %param.5) | copy-start | bytes 27652
  15.3 156.1 %reduce-scatter.5.cloned.1.call-start = ((), (), s32[]{:S(2)}) async-start(), calls=%async_computation.4 | async-start | bytes 2654208 | tf_op jit(solution)/shard_map/reduce_scatter | solution.py:27
Sparse Core Ops, SparseCore 0:
  14.8 50.4 reduce-scatter.2
Sparse Core Ops, SparseCore 1:
  17.4 81.8 all-gather.1
  102.6 68.8 reduce-scatter.4
where the time goes:
time: 181 us
  waiting for transfers between devices  105 us (58%)
  blocking collectives  39.4 us (22%)
  between operations  15.5 us (9%)
  matrix products  10.6 us (6%)
  other arithmetic  10.2 us (6%)
    reduce_scatter x1, waiting for transfers between devices, shards(): lax.psum_scatter(partial_value.astype(jnp.bfloat16), 'rep', scatter_dimen...  50 us
    psum x1, blocking collectives, shards(): gain_total = lax.psum(gain_local, ('rep', 'grp'))  39.4 us
    all_gather x1, waiting for transfers between devices, shards(): lax.all_gather(key_weight, 'grp', axis=0, tiled=True)  30.9 us
    reduce_scatter x1, waiting for transfers between devices, shards(): lax.psum_scatter(section_one, 'grp', scatter_dimension=0, tiled=True)  23.2 us
    dot_general x1, matrix products, shards(): lax.dot_general(key_grad, lax.all_gather(key_weight, 'grp', axis=0, tiled...  5.59 us
    dot_general x1, matrix products, shards(): lax.dot_general(normed, key_grad, (((0,), (0,)), ((), ())), preferred_ele...  4.97 us
  transfers between devices with their start and end apart: 3, of which 3 were waited for; matrix products, arithmetic and copies ran while one was open for 7% of the time, Pallas kernels for 0%

commit v1 on v0

--- a/solution.py
+++ b/solution.py
@@ -26,7 +26,8 @@
     ).astype(jnp.float32)
     weight_sum = lax.psum_scatter(section_one, "grp", scatter_dimension=0, tiled=True)
     gain_local = jnp.sum(d_normed * wide_tokens * inv_rms, axis=0)
-    gain_total = lax.psum(gain_local, ("rep", "grp"))
+    blocks = lax.all_gather(gain_local, ("rep", "grp"))
+    gain_total = jnp.sum(blocks, axis=0)
     scaled = d_normed * norm_gain
     inner_mean = jnp.mean(scaled * wide_tokens, axis=1, keepdims=True)
     token_grad = (inv_rms * (scaled - wide_tokens * inv_rms * inv_rms * inner_mean)).astype(

time: 181 us -> 187 us (1.033)
  blocking collectives: 39.4 us -> 68.2 us
  waiting for transfers between devices: 105 us -> 81.5 us
    all_gather x0 -> x1, blocking collectives: none -> 68.2 us  [shards(): blocks = lax.all_gather(gain_local, ('rep', 'grp'))]
    psum x1 -> x0, blocking collectives: 39.4 us -> none  [shards(): gain_total = lax.psum(gain_local, ('rep', 'grp'))]
    reduce_scatter x1, waiting for transfers between devices: 23.2 us -> 0.01 us  [shards(): lax.psum_scatter(section_one, 'grp', scatter_dimension=0, tiled=True)]
  transfers between devices with their start and end apart: 3 -> 3, of which waited for: 3 -> 2; matrix products, arithmetic and copies ran while one was open for 7% -> 7% of each run, Pallas kernels for 0% -> 0%
where the time goes in v1:
time: 187 us; the launch traced here: 186 us
  waiting for transfers between devices  81.5 us (44%)
  blocking collectives  68.2 us (36%)
  between operations  15.5 us (8%)
  matrix products  10.6 us (6%)
  other arithmetic  10.4 us (6%)
    all_gather x1, blocking collectives, shards(): blocks = lax.all_gather(gain_local, ('rep', 'grp'))  68.2 us
    reduce_scatter x1, waiting for transfers between devices, shards(): lax.psum_scatter(partial_value.astype(jnp.bfloat16), 'rep', scatter_dimen...  50 us
    all_gather x1, waiting for transfers between devices, shards(): lax.all_gather(key_weight, 'grp', axis=0, tiled=True)  30.9 us
    dot_general x1, matrix products, shards(): lax.dot_general(key_grad, lax.all_gather(key_weight, 'grp', axis=0, tiled...  5.59 us
    dot_general x1, matrix products, shards(): lax.dot_general(normed, key_grad, (((0,), (0,)), ((), ())), preferred_ele...  4.97 us
  transfers between devices with their start and end apart: 3, of which 2 were waited for; matrix products, arithmetic and copies ran while one was open for 7% of the time, Pallas kernels for 0%

profile of v1, /device:TPU:0, one launch (start us, length us, event | category | flops | bytes accessed | tf_op | source)
XLA Modules:
  0.0 186.3 jit_solution(14885376129136466503)
XLA Ops:
  8.0 0.0 copy-start
  8.0 0.0 reduce-scatter.3.cloned.1.call-start
  8.1 1.6 fusion.7
  9.7 0.0 copy-done
  9.7 5.0 %convolution_convert_fusion = bf16[2304,1024]{1,0:T(8,128)(2,1)} fusion(bf16[256,1024]{1,0:T(8,128)(2,1)S(1)} %copy-done, bf16[256,2304]{1,0:T(8,128)(2,1)} %param.4, f32[2304]{0:T(1024)} %param.5, f32[256]{0:T(256)S(1)} %add_rsqrt_fusion), kind=kOutput, calls=%fused_computation | convolution fusion | flops 1212678144 | bytes 6432768 | tf_op jit(solution)/shard_map/dot_general | solution.py:15
  14.7 0.0 reduce-scatter.3.cloned.1.call-update
  14.7 0.0 all-gather.4.cloned.1.call-start
  14.8 0.5 all-gather.4.cloned.1.call-update
  15.3 0.0 copy-start.1
  15.3 0.0 copy-start.2
  15.3 0.0 reduce-scatter.5.cloned.1.call-start
  15.4 50.0 %reduce-scatter.3.cloned.1.call-done = bf16[2304,256]{1,0:T(8,128)(2,1)} async-done(((bf16[2304,1024]{1,0:T(8,128)(2,1)}), bf16[2304,256]{1,0:T(8,128)(2,1)}) %reduce-scatter.3.cloned.1.call-update) | async-done | bytes 1179664 | tf_op jit(solution)/shard_map/reduce_scatter | solution.py:24
  65.3 2.9 %convert_element_type.19 = f32[2304,256]{1,0:T(8,128)} convert(bf16[2304,256]{1,0:T(8,128)(2,1)} %reduce-scatter.3.cloned.1.call-done) | non-fusion elementwise | flops 589824 | bytes 3538944 | tf_op jit(solution)/shard_map/convert_element_type | solution.py:26
  68.3 0.0 reduce-scatter.5.cloned.1.call-update
  68.3 30.9 %all-gather.4.cloned.1.call-done = bf16[2304,1024]{1,0:T(8,128)(2,1)} async-done(((bf16[288,1024]{1,0:T(8,128)(2,1)}), bf16[2304,1024]{1,0:T(8,128)(2,1)}) %all-gather.4.cloned.1.call-update) | async-done | bytes 4718608 | tf_op jit(solution)/shard_map/all_gather | solution.py:20
  99.2 0.0 copy-done.1
  99.2 0.0 copy-done.2
  99.2 5.6 %fusion.10 = (f32[2304]{0:T(1024)S(1)}, f32[256]{0:T(256)S(1)}, f32[256,2304]{1,0:T(8,128)}) fusion(bf16[256,2304]{1,0:T(8,128)(2,1)S(1)} %copy-done.1, f32[256]{0:T(256)S(1)} %add_rsqrt_fusion, f32[2304]{0:T(1024)S(1)} %copy-done.2, bf16[256,1024]{1,0:T(8,128)(2,1)S(1)} %copy-done, bf16[2304,1024]{1,0:T(8,128)(2,1)} %all-gather.4.cloned.1.call-done), kind=kOutput, calls=%fused_computation.15 | convolution fusion | flops 1212085760 | bytes 8802304 | tf_op jit(solution)/shard_map/dot_general | solution.py:18
  104.8 68.2 %all-gather.1 = f32[32,1,2304]{2,1,0:T(1,128)S(1)} all-gather(f32[1,1,2304]{2,1,0:T(1,128)S(1)} %reshape.20), channel_id=2, replica_groups=mesh['rep'=4,'grp'=8] {'rep','grp'}, dimensions={0}, use_global_device_ids=true | all-gather | bytes 304128 | tf_op jit(solution)/shard_map/all_gather | solution.py:29
  173.0 0.2 reduce_sum.39
  173.2 0.6 broadcast_multiply_fusion.1
  173.8 3.4 %fusion.5 = bf16[256,2304]{1,0:T(8,128)(2,1)} fusion(bf16[256,2304]{1,0:T(8,128)(2,1)S(1)} %copy-done.1, f32[256,2304]{1,0:T(8,128)} %get-tuple-element.5, f32[256]{0:T(256)S(1)} %broadcast_multiply_fusion.2, f32[2304]{0:T(1024)S(1)} %copy-done.2, f32[256]{0:T(256)S(1)} %add_rsqrt_fusion), kind=kLoop, calls=%fused_computation.10 | loop fusion | flops 4718592 | bytes 4729856 | tf_op jit(solution)/shard_map/convert_element_type | solution.py:33
  177.2 0.0 reduce-scatter.5.cloned.1.call-done
  177.2 1.7 broadcast_multiply_fusion
  (3 shorter events, 0.0 us)
Async XLA Ops:
  8.0 1.7 copy-start
  8.0 57.3 %reduce-scatter.3.cloned.1.call-start = ((), (), s32[]{:S(2)}) async-start(), calls=%async_computation.3 | async-start | bytes 5898240 | tf_op jit(solution)/shard_map/reduce_scatter | solution.py:24
  14.7 84.5 %all-gather.4.cloned.1.call-start = ((), (), s32[]{:S(2)}) async-start(), calls=%async_computation.2 | async-start | bytes 5308416 | tf_op jit(solution)/shard_map/all_gather | solution.py:20
  15.3 83.9 %copy-start.1 = (bf16[256,2304]{1,0:T(8,128)(2,1)S(1)}, bf16[256,2304]{1,0:T(8,128)(2,1)}, u32[]{:S(2)}) copy-start(bf16[256,2304]{1,0:T(8,128)(2,1)} %param.4) | copy-start | bytes 3538948
  15.3 83.9 %copy-start.2 = (f32[2304]{0:T(1024)S(1)}, f32[2304]{0:T(1024)}, u32[]{:S(2)}) copy-start(f32[2304]{0:T(1024)} %param.5) | copy-start | bytes 27652
  15.3 161.9 %reduce-scatter.5.cloned.1.call-start = ((), (), s32[]{:S(2)}) async-start(), calls=%async_computation.4 | async-start | bytes 2654208 | tf_op jit(solution)/shard_map/reduce_scatter | solution.py:27
Sparse Core Ops, SparseCore 0:
  14.8 50.4 reduce-scatter.2
Sparse Core Ops, SparseCore 1:
  17.4 81.8 all-gather.3
  102.6 69.1 reduce-scatter.4
